TPU v7x, 32 devices: a whole 2x2x4 slice. The times are simulated.
32 devices in a mesh: dp: 4 (over z), expert: 4 (over y, core), tensor: 2 (over x).
Axes of the slice: x: 2, y: 2, z: 4, core: 2. Of those that a mesh axis runs over, the one named last changes fastest.
Arguments:
- hidden: bfloat16 [2048, 6144], P(('dp', 'expert'), 'tensor'), may hold values from -6 to 6
- expert_ids: int32 [2048, 8], P(('dp', 'expert')), may hold values from 0 to 383, as said below
- gate_fixed: int32 [2048, 8], P(('dp', 'expert')), may hold values from 4096 to 65535
- slot_expert: int32 [16], replicated, may hold values from 0 to 383, as said below
- expert_in: bfloat16 [16, 6144, 2, 1024], P(('dp', 'expert'), 'tensor'), may hold values from -1 to 1, as said below
- expert_out: bfloat16 [16, 1024, 6144], P(('dp', 'expert'), None, 'tensor'), may hold values from -1 to 1, as said below
- shared_in: bfloat16 [6144, 2, 1024], P('tensor', None, 'dp'), may hold values from -0.078125 to 0.078125
- shared_out: bfloat16 [1024, 6144], P('dp', 'tensor'), may hold values from -0.1875 to 0.1875
Outputs:
- mixed: bfloat16 [2048, 6144], P(('dp', 'expert'), 'tensor')
Inputs may be any that keep to these rules, and one draw needn't show every extreme that they name: `expert_ids`: each row names 8 different experts. `slot_expert`: 14 different experts fill the 16 slots; 2 of them hold two slots each, the others one. `expert_in`: slots that hold the same expert hold the same weights. `expert_out`: slots that hold the same expert hold the same weights.
All inputs are finite; a program needn't handle non-finite values.
Results may differ from a plain program's by a relative error of at most 0.006.
Values may be sent and summed in bfloat16 or wider, within the bound.
A program may use at most 192 MiB of HBM per device.

v0:
```python
import jax
import jax.numpy as jnp
from jax import lax
from jax.sharding import PartitionSpec as P

EXPERTS = 384
CAP = 4
gate_scale = 1.0 / 65536.0


def swiglu(pre):
    return (jax.nn.silu(pre[:, 0, :]) * pre[:, 1, :]).astype(jnp.bfloat16)


def route_plan(chosen, row_rank, slot_expert):
    slot_count = slot_expert.shape[0]
    slot_iota = jnp.arange(slot_count, dtype=jnp.int32)[:, None]
    owns = slot_expert[:, None] == jnp.arange(chosen.shape[2], dtype=jnp.int32)[None, :]
    home = jnp.min(jnp.where(owns, slot_iota, slot_count), axis=0)
    spare = jnp.min(jnp.where(owns & (slot_iota != home[None, :]), slot_iota, slot_count), axis=0)
    home_of = jnp.sum(jnp.where(chosen, home[None, None, :], 0), axis=2)
    spare_of = jnp.sum(jnp.where(chosen, spare[None, None, :], 0), axis=2)
    first = row_rank < CAP
    spill = (row_rank >= CAP) & (row_rank < 2 * CAP) & (spare_of < slot_count)
    target = jnp.where(first, home_of, jnp.where(spill, spare_of, slot_count))
    slot_row = jnp.where(first, row_rank, row_rank - CAP)
    return (target, slot_row)


def dispatch_rows(send_rows):
    return lax.all_to_all(send_rows, ("dp", "expert"), split_axis=0, concat_axis=0, tiled=True)


def return_rows(answers):
    return lax.all_to_all(answers, ("dp", "expert"), split_axis=0, concat_axis=0, tiled=True)


def shards(
    hidden, expert_ids, gate_fixed, slot_expert, expert_in, expert_out, shared_in, shared_out
):
    tok_rows, half_width = hidden.shape
    topk_count = expert_ids.shape[1]
    slot_count = slot_expert.shape[0]
    experts_iota = jnp.arange(EXPERTS, dtype=jnp.int32)
    chosen = expert_ids[:, :, None] == experts_iota[None, None, :]
    picked = jnp.any(chosen, axis=1).astype(jnp.bfloat16)
    token_iota = jnp.arange(tok_rows, dtype=jnp.int32)
    earlier = (token_iota[:, None] > token_iota[None, :]).astype(jnp.bfloat16)
    before = jnp.dot(earlier, picked, preferred_element_type=jnp.float32)
    row_rank = jnp.sum(jnp.where(chosen, before[:, None, :], 0.0), axis=2).astype(jnp.int32)
    target, slot_row = route_plan(chosen, row_rank, slot_expert)
    flat_row = jnp.where(target < slot_count, target * CAP + slot_row, -1)
    row_iota = jnp.arange(slot_count * CAP, dtype=jnp.int32)
    owner = jnp.repeat(token_iota, topk_count)
    match_rows = flat_row.reshape(-1)[:, None] == row_iota[None, :]
    source_token = jnp.max(jnp.where(match_rows, owner[:, None], -1), axis=0)
    fetched_rows = jnp.take(hidden, jnp.maximum(source_token, 0), axis=0)
    send_rows = jnp.where(source_token[:, None] >= 0, fetched_rows, jnp.zeros((), jnp.bfloat16))
    piece = lax.all_gather(hidden, "dp", axis=0, tiled=True)
    partial_value = jnp.dot(
        piece, shared_in.reshape(half_width, -1), preferred_element_type=jnp.float32
    )
    shared_partial = partial_value.reshape(piece.shape[0], 2, -1)
    arrived = dispatch_rows(send_rows.reshape(slot_count, CAP, half_width))
    rows = arrived.reshape(-1, half_width)
    partial_value = jnp.dot(
        rows, expert_in[0].reshape(half_width, -1), preferred_element_type=jnp.float32
    )
    routed_partial = partial_value.reshape(rows.shape[0], 2, -1)
    shared_half, routed_half = (
        lax.psum_scatter(shared_partial, "tensor", scatter_dimension=2, tiled=True),
        lax.psum_scatter(routed_partial, "tensor", scatter_dimension=2, tiled=True),
    )
    shared_act, routed_act = (
        lax.all_gather(swiglu(shared_half), "tensor", axis=1, tiled=True),
        lax.all_gather(swiglu(routed_half), "tensor", axis=1, tiled=True),
    )
    shared_part = lax.psum_scatter(
        jnp.dot(shared_act, shared_out, preferred_element_type=jnp.float32),
        "dp",
        scatter_dimension=0,
        tiled=True,
    )
    answers = jnp.dot(routed_act, expert_out[0], preferred_element_type=jnp.float32).astype(
        jnp.bfloat16
    )
    returned = return_rows(answers.reshape(slot_count, CAP, half_width))
    returned = returned.reshape(-1, half_width)
    gates = gate_fixed.astype(jnp.float32) * gate_scale
    routed = jnp.zeros((tok_rows, half_width), jnp.float32)
    for column in range(topk_count):
        index = flat_row[:, column]
        answer_rows = jnp.take(returned, jnp.maximum(index, 0), axis=0).astype(jnp.float32)
        routed = routed + jnp.where(
            index[:, None] >= 0, gates[:, column : column + 1] * answer_rows, 0.0
        )
    return (shared_part + routed).astype(jnp.bfloat16)


def solution(mesh):
    in_specs = (
        P(("dp", "expert"), "tensor"),
        P(("dp", "expert"), None),
        P(("dp", "expert"), None),
        P(),
        P(("dp", "expert"), "tensor", None, None),
        P(("dp", "expert"), None, "tensor"),
        P("tensor", None, "dp"),
        P("dp", "tensor"),
    )
    out_specs = P(("dp", "expert"), "tensor")
    return jax.shard_map(shards, mesh=mesh, in_specs=in_specs, out_specs=out_specs, check_vma=False)
```

profile of v0, /device:TPU:8, one launch (start us, length us, event | category | flops | bytes accessed | tf_op | source)
XLA Modules:
  0.0 273.9 jit_solution(13360742678209995366)
XLA Ops:
  7.3 0.8 copy.22
  9.6 4.8 %select_reduce_fusion = (s32[128,8]{1,0:T(8,128)S(1)}, s32[128,8]{1,0:T(8,128)S(1)}) fusion(s32[384]{0:T(512)S(1)} %select_reduce_fusion.4, s32[128,8]{1,0:T(8,128)S(1)} %copy.22, s32[384]{0:T(512)S(1)} %select_reduce_fusion.5), kind=kLoop, calls=%fused_computation.15 | loop fusion | flops 1964032 | bytes 15360 | tf_op jit(solution)/shard_map/reduce_sum | solution.py:22
  16.3 0.8 gather_fusion
  17.2 4.4 %copy.24 = bf16[384,8,2,256]{3,1,2,0:T(8,128)(2,1)} copy(bf16[384,8,2,256]{3,2,1,0:T(2,128)(2,1)} %bitcast.66) | data formatting | bytes 6291456
  21.6 4.7 %copy.21 = bf16[512,3072]{1,0:T(8,128)(2,1)} copy(bf16[512,3072]{0,1:T(8,128)(2,1)} %bitcast.65) | data formatting | bytes 6291456 | tf_op jit(solution)/shard_map/dot_general | solution.py:60
  26.3 45.1 %all-gather.2.cloned.1.call-done = bf16[512,3072]{1,0:T(8,128)(2,1)} async-done(((bf16[128,3072]{1,0:T(8,128)(2,1)}), bf16[512,3072]{1,0:T(8,128)(2,1)}) %all-gather.2.cloned.1.call-update) | async-done | bytes 3145744 | tf_op jit(solution)/shard_map/all_gather | solution.py:59
  71.4 5.7 %fusion.5 = f32[512,2,256]{2,0,1:T(8,128)} fusion(bf16[2,256,3072]{2,1,0:T(8,128)(2,1)} %bitcast.67, bf16[512,3072]{1,0:T(8,128)(2,1)} %all-gather.2.cloned.1.call-done), kind=kOutput, calls=%fused_computation.12 | convolution fusion | flops 1610612736 | bytes 7340032 | tf_op jit(solution)/shard_map/dot_general | solution.py:60
  77.1 1.1 select_select_fusion
  78.2 6.1 %all-to-all-start = ((bf16[16,4,3072]{2,1,0:T(4,128)(2,1)}), bf16[16,4,3072]{2,1,0:T(4,128)(2,1)S(1)}, u32[]{:S(2)}, u32[]{:S(2)}) async-start(bf16[16,4,3072]{2,1,0:T(4,128)(2,1)} %select_select_fusion), calls=%async_computation.2 | async-start | bytes 786432 | tf_op jit(solution)/shard_map/all_to_all | solution.py:31
  84.6 13.0 %copy.25 = bf16[384,8,2,1024]{3,1,2,0:T(8,128)(2,1)} copy(bf16[384,8,2,1024]{3,2,1,0:T(2,128)(2,1)} %bitcast.64) | data formatting | bytes 25165824
  97.6 16.7 %copy.23 = bf16[2048,3072]{1,0:T(8,128)(2,1)} copy(bf16[2048,3072]{0,1:T(8,128)(2,1)} %bitcast.63) | data formatting | bytes 25165824 | tf_op jit(solution)/shard_map/dot_general | solution.py:66
  114.3 9.3 %fusion.19 = f32[64,2,1024]{2,0,1:T(8,128)} fusion(bf16[64,3072,1]{1,0,2:T(8,128)(2,1)S(1)} %reshape.214, bf16[2,1024,3072]{2,1,0:T(8,128)(2,1)} %bitcast.62), kind=kOutput, calls=%fused_computation.100 | convolution fusion | flops 805306368 | bytes 13500416 | tf_op jit(solution)/shard_map/dot_general | solution.py:66
  123.7 1.1 fusion.9
  124.8 6.2 %all_gather.10 = bf16[512,256]{1,0:T(8,128)(2,1)S(1)} all-gather(bf16[512,128]{1,0:T(8,128)(2,1)S(1)} %fusion.9), channel_id=1, replica_groups=mesh['dp'=4,'expert'=4,'tensor'=2] {'tensor'}, dimensions={1}, use_global_device_ids=true | all-gather | bytes 393216 | tf_op jit(solution)/shard_map/all_gather | solution.py:75
  131.1 3.7 %fusion.18 = f32[512,3072]{1,0:T(8,128)} fusion(bf16[512,256]{1,0:T(8,128)(2,1)S(1)} %all_gather.10, bf16[256,3072]{1,0:T(8,128)(2,1)S(1)} %copy-done), kind=kOutput, calls=%fused_computation.99 | convolution fusion | flops 805306368 | bytes 8126464 | tf_op jit(solution)/shard_map/dot_general | solution.py:79
  135.8 3.6 %reduce-scatter.8.cloned.1.call-done = f32[64,2,512]{2,0,1:T(8,128)} async-done(((f32[64,2,1024]{2,0,1:T(8,128)}), f32[64,2,512]{2,0,1:T(8,128)}) %reduce-scatter.8.cloned.1.call-update) | async-done | bytes 262160 | tf_op jit(solution)/shard_map/reduce_scatter | solution.py:72
  139.3 1.0 fusion.11
  140.4 4.9 %all_gather.11 = bf16[64,1024]{1,0:T(8,128)(2,1)S(1)} all-gather(bf16[64,512]{1,0:T(8,128)(2,1)S(1)} %fusion.11), channel_id=1, replica_groups=mesh['dp'=4,'expert'=4,'tensor'=2] {'tensor'}, dimensions={1}, use_global_device_ids=true | all-gather | bytes 196608 | tf_op jit(solution)/shard_map/all_gather | solution.py:76
  145.3 4.2 %fusion.2 = bf16[64,3072]{1,0:T(8,128)(2,1)S(1)} fusion(bf16[64,1024]{1,0:T(8,128)(2,1)S(1)} %all_gather.11, bf16[1,1024,3072]{2,1,0:T(8,128)(2,1)} %param.15), kind=kOutput, calls=%fused_computation.11 | convolution fusion | flops 402849792 | bytes 6815744 | tf_op jit(solution)/shard_map/dot_general | solution.py:84
  149.6 0.9 reshape.114
  150.5 6.1 %all-to-all-start.1 = ((bf16[16,4,3072]{2,1,0:T(4,128)(2,1)}), bf16[16,4,3072]{2,1,0:T(4,128)(2,1)S(1)}, u32[]{:S(2)}, u32[]{:S(2)}) async-start(bf16[16,4,3072]{2,1,0:T(4,128)(2,1)} %reshape.114), calls=%async_computation.4 | async-start | bytes 786432 | tf_op jit(solution)/shard_map/all_to_all | solution.py:35
  156.6 23.3 %all-to-all-done.1 = bf16[16,4,3072]{2,1,0:T(4,128)(2,1)S(1)} async-done(((bf16[16,4,3072]{2,1,0:T(4,128)(2,1)}), bf16[16,4,3072]{2,1,0:T(4,128)(2,1)S(1)}, u32[]{:S(2)}, u32[]{:S(2)}) %all-to-all-start.1) | async-done | bytes 393248 | tf_op jit(solution)/shard_map/all_to_all | solution.py:35
  180.0 1.0 gather_fusion.2
  181.0 1.0 gather_fusion.3
  182.1 2.0 gather_fusion.4
  184.0 1.9 gather_fusion.5
  186.0 2.0 gather_fusion.6
  188.0 2.0 gather_fusion.7
  189.9 1.9 gather_fusion.8
  191.8 1.9 gather_fusion.1
  193.8 67.0 %reduce-scatter.6.cloned.1.call-done = f32[128,3072]{1,0:T(8,128)} async-done(((f32[512,3072]{1,0:T(8,128)}), f32[128,3072]{1,0:T(8,128)}) %reduce-scatter.6.cloned.1.call-update) | async-done | bytes 1572880 | tf_op jit(solution)/shard_map/reduce_scatter | solution.py:78
  260.8 6.6 %add_convert_fusion = bf16[128,3072]{1,0:T(8,128)(2,1)} fusion(f32[128,3072]{1,0:T(8,128)} %reduce-scatter.6.cloned.1.call-done, bf16[128,3072]{1,0:T(8,128)(2,1)} %gather_fusion.8, bf16[128,3072]{1,0:T(8,128)(2,1)} %gather_fusion.7, bf16[128,3072]{1,0:T(8,128)(2,1)} %gather_fusion.6, bf16[128,3072]{1,0:T(8,128)(2,1)} %gather_fusion.5, ...), kind=kLoop, calls=%fused_computation.14 | loop fusion | flops 16121856 | bytes 8656896 | tf_op jit(solution)/shard_map/convert_element_type | solution.py:97
  (60 shorter events, 5.6 us)
Async XLA Ops:
  6.5 124.5 %copy-start = (bf16[256,3072]{1,0:T(8,128)(2,1)S(1)}, bf16[256,3072]{1,0:T(8,128)(2,1)}, u32[]{:S(2)}) copy-start(bf16[256,3072]{1,0:T(8,128)(2,1)} %param.17) | copy-start | bytes 4718596
  6.5 9.7 %copy-start.2 = (bf16[128,3072]{1,0:T(8,128)(2,1)S(1)}, bf16[128,3072]{1,0:T(8,128)(2,1)}, u32[]{:S(2)}) copy-start(bf16[128,3072]{1,0:T(8,128)(2,1)} %param.10) | copy-start | bytes 2359300
  6.5 64.8 %all-gather.2.cloned.1.call-start = ((), (), s32[]{:S(2)}) async-start(), calls=%async_computation.5 | async-start | bytes 3932160 | tf_op jit(solution)/shard_map/all_gather | solution.py:59
  7.3 116.5 %reduce-scatter.4.cloned.1.call-start = ((), (), s32[]{:S(2)}) async-start(), calls=%async_computation.6 | async-start | bytes 1572864 | tf_op jit(solution)/shard_map/reduce_scatter | solution.py:71
  78.2 36.0 %all-to-all-start = ((bf16[16,4,3072]{2,1,0:T(4,128)(2,1)}), bf16[16,4,3072]{2,1,0:T(4,128)(2,1)S(1)}, u32[]{:S(2)}, u32[]{:S(2)}) async-start(bf16[16,4,3072]{2,1,0:T(4,128)(2,1)} %select_select_fusion), calls=%async_computation.2 | async-start | bytes 786432 | tf_op jit(solution)/shard_map/all_to_all | solution.py:31
  84.3 55.0 %reduce-scatter.8.cloned.1.call-start = ((), (), s32[]{:S(2)}) async-start(), calls=%async_computation.8 | async-start | bytes 786432 | tf_op jit(solution)/shard_map/reduce_scatter | solution.py:72
  123.6 137.1 %reduce-scatter.6.cloned.1.call-start = ((), (), s32[]{:S(2)}) async-start(), calls=%async_computation.7 | async-start | bytes 7864320 | tf_op jit(solution)/shard_map/reduce_scatter | solution.py:78
  149.5 7.0 %copy-start.3 = (s32[128,8]{0,1:T(8,128)S(1)}, s32[128,8]{0,1:T(8,128)}, u32[]{:S(2)}) copy-start(s32[128,8]{0,1:T(8,128)} %param.12) | copy-start | bytes 12292
  150.5 29.4 %all-to-all-start.1 = ((bf16[16,4,3072]{2,1,0:T(4,128)(2,1)}), bf16[16,4,3072]{2,1,0:T(4,128)(2,1)S(1)}, u32[]{:S(2)}, u32[]{:S(2)}) async-start(bf16[16,4,3072]{2,1,0:T(4,128)(2,1)} %reshape.114), calls=%async_computation.4 | async-start | bytes 786432 | tf_op jit(solution)/shard_map/all_to_all | solution.py:35
  260.8 6.6 %copy-start.1 = (bf16[256,3072]{1,0:T(8,128)(2,1)S(1)}, bf16[256,3072]{1,0:T(8,128)(2,1)}, u32[]{:S(2)}) copy-start(bf16[256,3072]{1,0:T(8,128)(2,1)} %param.17) | copy-start | bytes 4718596
Sparse Core Ops, SparseCore 0:
  8.9 62.4 all-gather.1
  77.2 21.2 reduce-scatter.3
  123.8 15.5 reduce-scatter.7
  141.5 119.2 reduce-scatter.5
where the time goes:
time: 275 us; the launch traced here: 274 us
  waiting for transfers between devices  140 us (51%)
  local copies, waits for them, and re-layouts  55.9 us (20%)
  matrix products  23.1 us (8%)
  other arithmetic  18 us (7%)
  between operations  13.4 us (5%)
  starting transfers between devices  12.5 us (5%)
  blocking collectives  11.2 us (4%)
    reduce_scatter x1, waiting for transfers between devices, shards(): lax.psum_scatter(jnp.dot(shared_act, shared_out, preferred_element_type=j...  67 us
    all_gather x1, waiting for transfers between devices, shards(): piece = lax.all_gather(hidden, 'dp', axis=0, tiled=True)  45.1 us
    all_to_all x1, waiting for transfers between devices, return_rows(): lax.all_to_all(answers, ('dp', 'expert'), split_axis=0, concat_axis=0, ti...  23.3 us
    unnamed x11, local copies, waits for them, and re-layouts  18.2 us
    dot_general x1, local copies, waits for them, and re-layouts, shards(): jnp.dot(rows, expert_in[0].reshape(half_width, -1), preferred_element_typ...  16.7 us
    gather x8, local copies, waits for them, and re-layouts, shards(): jnp.take(returned, jnp.maximum(index, 0), axis=0).astype(jnp.float32)  13.8 us
    dot_general x1, matrix products, shards(): jnp.dot(rows, expert_in[0].reshape(half_width, -1), preferred_element_typ...  9.29 us
    convert_element_type x1, other arithmetic, shards(): return (shared_part + routed).astype(jnp.bfloat16)  6.55 us
  transfers between devices with their start and end apart: 6, of which 4 were waited for; matrix products, arithmetic and copies ran while one was open for 31% of the time, Pallas kernels for 0%

commit v1 on v0

--- a/solution.py
+++ b/solution.py
@@ -56,7 +56,14 @@
     source_token = jnp.max(jnp.where(match_rows, owner[:, None], -1), axis=0)
     fetched_rows = jnp.take(hidden, jnp.maximum(source_token, 0), axis=0)
     send_rows = jnp.where(source_token[:, None] >= 0, fetched_rows, jnp.zeros((), jnp.bfloat16))
-    piece = lax.all_gather(hidden, "dp", axis=0, tiled=True)
+    peers = lax.axis_size("dp")
+    right = [(i, (i + 1) % peers) for i in range(peers)]
+    parts = [hidden]
+    for stride in range(1, peers):
+        parts = [lax.ppermute(parts[0], "dp", right), *parts]
+    result = jnp.concatenate(parts, axis=0)
+    turn = (lax.axis_index("dp") + 1) * parts[-1].shape[0]
+    piece = jnp.roll(result, turn, axis=0)
     partial_value = jnp.dot(
         piece, shared_in.reshape(half_width, -1), preferred_element_type=jnp.float32
     )

time: 275 us -> 274 us (level)
  waiting for transfers between devices: 140 us -> 127 us
  local copies, waits for them, and re-layouts: 55.9 us -> 65.5 us
  starting transfers between devices: 12.5 us -> 17.1 us
  matrix products: 23.1 us -> 20.1 us
    all_gather x1 -> x0, waiting for transfers between devices: 45.1 us -> none  [shards(): piece = lax.all_gather(hidden, 'dp', axis=0, tiled=True)]
    ppermute x0 -> x3, waiting for transfers between devices: none -> 34 us  [shards(): parts = [lax.ppermute(parts[0], 'dp', right), *parts]]
    unnamed x11 -> x32, local copies, waits for them, and re-layouts: 18.2 us -> 26.1 us
    ppermute x0 -> x3, starting transfers between devices: none -> 3.85 us  [shards(): parts = [lax.ppermute(parts[0], 'dp', right), *parts]]
    dot_general x1, matrix products: 5.73 us -> 2.89 us  [shards(): jnp.dot(piece, shared_in.reshape(half_width, -1), preferred_element_type=...]
  transfers between devices with their start and end apart: 6 -> 8, of which waited for: 4 -> 6; matrix products, arithmetic and copies ran while one was open for 31% -> 32% of each run, Pallas kernels for 0% -> 0%
where the time goes in v1:
time: 274 us; the launch traced here: 272 us
  waiting for transfers between devices  127 us (46%)
  local copies, waits for them, and re-layouts  65.5 us (24%)
  matrix products  20.1 us (7%)
  other arithmetic  18.1 us (7%)
  starting transfers between devices  17.1 us (6%)
  between operations  13.5 us (5%)
  blocking collectives  11.2 us (4%)
    reduce_scatter x1, waiting for transfers between devices, shards(): lax.psum_scatter(jnp.dot(shared_act, shared_out, preferred_element_type=j...  67.2 us
    ppermute x3, waiting for transfers between devices, shards(): parts = [lax.ppermute(parts[0], 'dp', right), *parts]  34 us
    unnamed x32, local copies, waits for them, and re-layouts  26.1 us
    all_to_all x1, waiting for transfers between devices, return_rows(): lax.all_to_all(answers, ('dp', 'expert'), split_axis=0, concat_axis=0, ti...  23.4 us
    dot_general x1, local copies, waits for them, and re-layouts, shards(): jnp.dot(rows, expert_in[0].reshape(half_width, -1), preferred_element_typ...  16.6 us
    gather x8, local copies, waits for them, and re-layouts, shards(): jnp.take(returned, jnp.maximum(index, 0), axis=0).astype(jnp.float32)  13.8 us
    dot_general x1, matrix products, shards(): jnp.dot(rows, expert_in[0].reshape(half_width, -1), preferred_element_typ...  9.29 us
    all_to_all x1, starting transfers between devices, dispatch_rows(): lax.all_to_all(send_rows, ('dp', 'expert'), split_axis=0, concat_axis=0,...  6.91 us
  transfers between devices with their start and end apart: 8, of which 6 were waited for; matrix products, arithmetic and copies ran while one was open for 32% of the time, Pallas kernels for 0%

profile of v1, /device:TPU:8, one launch (start us, length us, event | category | flops | bytes accessed | tf_op | source)
XLA Modules:
  0.0 272.4 jit_solution(13596095282612889563)
XLA Ops:
  6.5 1.6 collective-permute-start
  9.6 16.4 %collective-permute-done = bf16[128,3072]{1,0:T(8,128)(2,1)S(1)} collective-permute-done((bf16[128,3072]{1,0:T(8,128)(2,1)}, bf16[128,3072]{1,0:T(8,128)(2,1)S(1)}, u32[]{:S(2)}, u32[]{:S(2)}) %collective-permute-start) | collective-permute-done | bytes 786464 | tf_op jit(solution)/shard_map/ppermute | solution.py:63
  26.0 1.6 collective-permute-start.1
  28.4 4.8 %select_reduce_fusion = (s32[128,8]{1,0:T(8,128)S(1)}, s32[128,8]{1,0:T(8,128)S(1)}) fusion(s32[384]{0:T(512)S(1)} %select_reduce_fusion.4, s32[128,8]{1,0:T(8,128)S(1)} %copy.22, s32[384]{0:T(512)S(1)} %select_reduce_fusion.5), kind=kLoop, calls=%fused_computation.16 | loop fusion | flops 1964032 | bytes 15360 | tf_op jit(solution)/shard_map/reduce_sum | solution.py:22
  35.2 10.3 %collective-permute-done.1 = bf16[128,3072]{1,0:T(8,128)(2,1)} collective-permute-done((bf16[128,3072]{1,0:T(8,128)(2,1)S(1)}, bf16[128,3072]{1,0:T(8,128)(2,1)}, u32[]{:S(2)}, u32[]{:S(2)}) %collective-permute-start.1) | collective-permute-done | bytes 786464 | tf_op jit(solution)/shard_map/ppermute | solution.py:63
  46.7 1.5 gather_fusion
  49.3 4.1 %copy.24 = bf16[384,8,2,256]{3,1,2,0:T(8,128)(2,1)} copy(bf16[384,8,2,256]{3,2,1,0:T(2,128)(2,1)} %bitcast.66) | data formatting | bytes 6291456
  53.5 4.6 %copy.21 = bf16[512,3072]{1,0:T(8,128)(2,1)} copy(bf16[512,3072]{0,1:T(8,128)(2,1)} %bitcast.65) | data formatting | bytes 6291456 | tf_op jit(solution)/shard_map/dot_general | solution.py:67
  58.1 7.3 %collective-permute-done.2 = bf16[128,3072]{1,0:T(8,128)(2,1)} collective-permute-done((bf16[128,3072]{1,0:T(8,128)(2,1)}, bf16[128,3072]{1,0:T(8,128)(2,1)}, u32[]{:S(2)}, u32[]{:S(2)}) %collective-permute-start.2) | collective-permute-done | bytes 786464 | tf_op jit(solution)/shard_map/ppermute | solution.py:63
  66.6 1.2 constant_dynamic-update-slice_fusion.6
  67.9 1.2 constant_dynamic-update-slice_fusion.3
  70.4 1.8 copy-done.3
  72.2 2.9 %fusion.5 = f32[512,2,256]{2,0,1:T(8,128)} fusion(bf16[2,256,3072]{2,1,0:T(8,128)(2,1)S(1)} %bitcast.67, bf16[1024,3072]{1,0:T(8,128)(2,1)S(1)} %constant_dynamic-update-slice_fusion, s32[]{:T(128)S(6)} %select_n.119), kind=kOutput, calls=%fused_computation.12 | convolution fusion | flops 1610612736 | bytes 7340036 | tf_op jit(solution)/shard_map/dot_general | solution.py:67
  76.2 6.9 %all-to-all-start = ((bf16[16,4,3072]{2,1,0:T(4,128)(2,1)}), bf16[16,4,3072]{2,1,0:T(4,128)(2,1)S(1)}, u32[]{:S(2)}, u32[]{:S(2)}) async-start(bf16[16,4,3072]{2,1,0:T(4,128)(2,1)} %select_select_fusion), calls=%async_computation.2 | async-start | bytes 786432 | tf_op jit(solution)/shard_map/all_to_all | solution.py:31
  83.4 13.0 %copy.25 = bf16[384,8,2,1024]{3,1,2,0:T(8,128)(2,1)} copy(bf16[384,8,2,1024]{3,2,1,0:T(2,128)(2,1)} %bitcast.64) | data formatting | bytes 25165824
  96.4 16.6 %copy.23 = bf16[2048,3072]{1,0:T(8,128)(2,1)} copy(bf16[2048,3072]{0,1:T(8,128)(2,1)} %bitcast.63) | data formatting | bytes 25165824 | tf_op jit(solution)/shard_map/dot_general | solution.py:73
  113.1 9.3 %fusion.21 = f32[64,2,1024]{2,0,1:T(8,128)} fusion(bf16[64,3072,1]{1,0,2:T(8,128)(2,1)S(1)} %reshape.214, bf16[2,1024,3072]{2,1,0:T(8,128)(2,1)} %bitcast.62), kind=kOutput, calls=%fused_computation.110 | convolution fusion | flops 805306368 | bytes 13500416 | tf_op jit(solution)/shard_map/dot_general | solution.py:73
  123.6 6.2 %all_gather.6 = bf16[512,256]{1,0:T(8,128)(2,1)S(1)} all-gather(bf16[512,128]{1,0:T(8,128)(2,1)S(1)} %fusion.10), channel_id=1, replica_groups=mesh['dp'=4,'expert'=4,'tensor'=2] {'tensor'}, dimensions={1}, use_global_device_ids=true | all-gather | bytes 393216 | tf_op jit(solution)/shard_map/all_gather | solution.py:82
  129.9 3.7 %fusion.20 = f32[512,3072]{1,0:T(8,128)} fusion(bf16[512,256]{1,0:T(8,128)(2,1)S(1)} %all_gather.6, bf16[256,3072]{1,0:T(8,128)(2,1)S(1)} %copy-done), kind=kOutput, calls=%fused_computation.109 | convolution fusion | flops 805306368 | bytes 8126464 | tf_op jit(solution)/shard_map/dot_general | solution.py:86
  135.4 2.4 reduce-scatter.8.cloned.1.call-done
  138.8 4.9 %all_gather.7 = bf16[64,1024]{1,0:T(8,128)(2,1)S(1)} all-gather(bf16[64,512]{1,0:T(8,128)(2,1)S(1)} %fusion.12), channel_id=1, replica_groups=mesh['dp'=4,'expert'=4,'tensor'=2] {'tensor'}, dimensions={1}, use_global_device_ids=true | all-gather | bytes 196608 | tf_op jit(solution)/shard_map/all_gather | solution.py:83
  143.7 4.1 %fusion.2 = bf16[64,3072]{1,0:T(8,128)(2,1)S(1)} fusion(bf16[64,1024]{1,0:T(8,128)(2,1)S(1)} %all_gather.7, bf16[1,1024,3072]{2,1,0:T(8,128)(2,1)} %param.15), kind=kOutput, calls=%fused_computation.11 | convolution fusion | flops 402849792 | bytes 6815744 | tf_op jit(solution)/shard_map/dot_general | solution.py:91
  148.8 6.0 %all-to-all-start.1 = ((bf16[16,4,3072]{2,1,0:T(4,128)(2,1)}), bf16[16,4,3072]{2,1,0:T(4,128)(2,1)S(1)}, u32[]{:S(2)}, u32[]{:S(2)}) async-start(bf16[16,4,3072]{2,1,0:T(4,128)(2,1)} %reshape.114), calls=%async_computation.4 | async-start | bytes 786432 | tf_op jit(solution)/shard_map/all_to_all | solution.py:35
  154.9 23.4 %all-to-all-done.1 = bf16[16,4,3072]{2,1,0:T(4,128)(2,1)S(1)} async-done(((bf16[16,4,3072]{2,1,0:T(4,128)(2,1)}), bf16[16,4,3072]{2,1,0:T(4,128)(2,1)S(1)}, u32[]{:S(2)}, u32[]{:S(2)}) %all-to-all-start.1) | async-done | bytes 393248 | tf_op jit(solution)/shard_map/all_to_all | solution.py:35
  180.4 1.9 gather_fusion.6
  182.3 2.0 gather_fusion.5
  184.3 2.0 gather_fusion.4
  186.3 1.9 gather_fusion.3
  188.2 2.0 gather_fusion.2
  190.2 1.9 gather_fusion.1
  192.1 67.2 %reduce-scatter.6.cloned.1.call-done = f32[128,3072]{1,0:T(8,128)} async-done(((f32[512,3072]{1,0:T(8,128)}), f32[128,3072]{1,0:T(8,128)}) %reduce-scatter.6.cloned.1.call-update) | async-done | bytes 1572880 | tf_op jit(solution)/shard_map/reduce_scatter | solution.py:85
  259.3 6.6 %add_convert_fusion = bf16[128,3072]{1,0:T(8,128)(2,1)} fusion(f32[128,3072]{1,0:T(8,128)} %reduce-scatter.6.cloned.1.call-done, bf16[128,3072]{1,0:T(8,128)(2,1)S(1)} %gather_fusion.8, bf16[128,3072]{1,0:T(8,128)(2,1)S(1)} %gather_fusion.7, bf16[128,3072]{1,0:T(8,128)(2,1)} %gather_fusion.6, bf16[128,3072]{1,0:T(8,128)(2,1)} %gather_fusion.5, ...), kind=kLoop, calls=%fused_computation.15 | loop fusion | flops 16121856 | bytes 8656896 | tf_op jit(solution)/shard_map/convert_element_type | solution.py:104
  (85 shorter events, 17.7 us)
Async XLA Ops:
  6.5 123.3 %copy-start = (bf16[256,3072]{1,0:T(8,128)(2,1)S(1)}, bf16[256,3072]{1,0:T(8,128)(2,1)}, u32[]{:S(2)}) copy-start(bf16[256,3072]{1,0:T(8,128)(2,1)} %param.17) | copy-start | bytes 4718596
  6.5 40.1 %copy-start.2 = (bf16[128,3072]{1,0:T(8,128)(2,1)S(1)}, bf16[128,3072]{1,0:T(8,128)(2,1)}, u32[]{:S(2)}) copy-start(bf16[128,3072]{1,0:T(8,128)(2,1)} %param.10) | copy-start | bytes 2359300
  6.5 116.0 %reduce-scatter.4.cloned.1.call-start = ((), (), s32[]{:S(2)}) async-start(), calls=%async_computation.5 | async-start | bytes 1572864 | tf_op jit(solution)/shard_map/reduce_scatter | solution.py:78
  6.5 19.5 %collective-permute-start = (bf16[128,3072]{1,0:T(8,128)(2,1)}, bf16[128,3072]{1,0:T(8,128)(2,1)S(1)}, u32[]{:S(2)}, u32[]{:S(2)}) collective-permute-start(bf16[128,3072]{1,0:T(8,128)(2,1)} %param.10), channel_id=1, source_target_pairs={{0,8},{8,16},{16,24},{24,0},{1,9},{9,17},{17,25},{25,1},{2,10},{10... | collective-permute-start | bytes 2359304 | tf_op jit(solution)/shard_map/ppermute | solution.py:63
  26.0 19.4 %collective-permute-start.1 = (bf16[128,3072]{1,0:T(8,128)(2,1)S(1)}, bf16[128,3072]{1,0:T(8,128)(2,1)}, u32[]{:S(2)}, u32[]{:S(2)}) collective-permute-start(bf16[128,3072]{1,0:T(8,128)(2,1)S(1)} %collective-permute-done), channel_id=1, source_target_pairs={{0,8},{8,16},{16,24},{24,0},{1,9},{9,17},{17,25},{25,1},{2,10},{10... | collective-permute-start | bytes 2359304 | tf_op jit(solution)/shard_map/ppermute | solution.py:63
  33.1 13.5 %copy-start.4 = (s32[128,8]{1,0:T(8,128)}, s32[128,8]{1,0:T(8,128)S(1)}, u32[]{:S(2)}) copy-start(s32[128,8]{1,0:T(8,128)S(1)} %get-tuple-element.22) | copy-start | bytes 12292
  33.1 13.5 %copy-start.6 = (s32[128,8]{1,0:T(8,128)}, s32[128,8]{1,0:T(8,128)S(1)}, u32[]{:S(2)}) copy-start(s32[128,8]{1,0:T(8,128)S(1)} %get-tuple-element.23) | copy-start | bytes 12292
  34.4 0.6 copy-start.8
  45.4 20.0 %collective-permute-start.2 = (bf16[128,3072]{1,0:T(8,128)(2,1)}, bf16[128,3072]{1,0:T(8,128)(2,1)}, u32[]{:S(2)}, u32[]{:S(2)}) collective-permute-start(bf16[128,3072]{1,0:T(8,128)(2,1)} %collective-permute-done.1), channel_id=1, source_target_pairs={{0,8},{8,16},{16,24},{24,0},{1,9},{9,17},{17,25},{25,1},{2,10},{10... | collective-permute-start | bytes 2359304 | tf_op jit(solution)/shard_map/ppermute | solution.py:63
  70.3 1.9 copy-start.3
  76.2 36.8 %all-to-all-start = ((bf16[16,4,3072]{2,1,0:T(4,128)(2,1)}), bf16[16,4,3072]{2,1,0:T(4,128)(2,1)S(1)}, u32[]{:S(2)}, u32[]{:S(2)}) async-start(bf16[16,4,3072]{2,1,0:T(4,128)(2,1)} %select_select_fusion), calls=%async_computation.2 | async-start | bytes 786432 | tf_op jit(solution)/shard_map/all_to_all | solution.py:31
  83.1 54.6 %reduce-scatter.8.cloned.1.call-start = ((), (), s32[]{:S(2)}) async-start(), calls=%async_computation.7 | async-start | bytes 786432 | tf_op jit(solution)/shard_map/reduce_scatter | solution.py:79
  122.4 136.9 %reduce-scatter.6.cloned.1.call-start = ((), (), s32[]{:S(2)}) async-start(), calls=%async_computation.6 | async-start | bytes 7864320 | tf_op jit(solution)/shard_map/reduce_scatter | solution.py:85
  133.5 0.8 copy-start.5
  133.5 0.9 copy-start.7
  133.5 0.9 copy-start.9
  147.8 7.0 %copy-start.10 = (s32[128,8]{0,1:T(8,128)S(1)}, s32[128,8]{0,1:T(8,128)}, u32[]{:S(2)}) copy-start(s32[128,8]{0,1:T(8,128)} %param.12) | copy-start | bytes 12292
  148.8 29.5 %all-to-all-start.1 = ((bf16[16,4,3072]{2,1,0:T(4,128)(2,1)}), bf16[16,4,3072]{2,1,0:T(4,128)(2,1)S(1)}, u32[]{:S(2)}, u32[]{:S(2)}) async-start(bf16[16,4,3072]{2,1,0:T(4,128)(2,1)} %reshape.114), calls=%async_computation.4 | async-start | bytes 786432 | tf_op jit(solution)/shard_map/all_to_all | solution.py:35
  259.3 6.6 %copy-start.1 = (bf16[256,3072]{1,0:T(8,128)(2,1)S(1)}, bf16[256,3072]{1,0:T(8,128)(2,1)}, u32[]{:S(2)}) copy-start(bf16[256,3072]{1,0:T(8,128)(2,1)} %param.17) | copy-start | bytes 4718596
Sparse Core Ops, SparseCore 0:
  75.2 21.2 reduce-scatter.3
  122.6 15.1 reduce-scatter.7
  140.1 119.1 reduce-scatter.5
